TPU v7x, 512 devices: a whole 4x4x16 slice. The times are simulated.
512 devices in a mesh: lon: 16 (over z_hi, x, core), lat: 32 (over z_lo, y).
Axes of the slice: x: 4, y: 4, z: 16 (z_hi: 2, z_lo: 8; z = z_hi * 8 + z_lo), core: 2. Of those that a mesh axis runs over, the one named last changes fastest.
Arguments:
- u_vel: float32 [16, 512, 4320], P(None, 'lat', 'lon'), may hold values from -6 to 6
- v_vel: float32 [16, 512, 4320], P(None, 'lat', 'lon'), may hold values from -6 to 6
- u_mask: int32 [16, 512, 4320], P(None, 'lat', 'lon'), may hold values 0 or 1
- v_mask: int32 [16, 512, 4320], P(None, 'lat', 'lon'), may hold values 0 or 1
- t_mask: int32 [16, 512, 4320], P(None, 'lat', 'lon'), may hold values 0 or 1
- bottom: int32 [512, 4320], P('lat', 'lon'), may hold values from 0 to 16
- inv_dx: float32 [512, 4320], P('lat', 'lon'), may hold values from 0.5 to 2
- inv_dy: float32 [512, 4320], P('lat', 'lon'), may hold values from 0.5 to 2
Outputs:
- flux_spectrum: float32 [16, 512, 2160], P(None, ('lat', 'lon'))
All inputs are finite; a program needn't handle non-finite values. No bound on the sum of `u_mask` or of `v_mask` or of `t_mask` on one device may be relied on, other than what follows from the above.
Results may differ from a plain program's by a relative error of at most 0.0003.
Values sent between devices are 32-bit elements; how exact they have to be, the bound alone decides.
No kernel may reach another device: no remote copies, remote signals or barrier semaphores. Data moves between devices by JAX's collectives and lax.ppermute only.
A program may use at most 64 MiB of HBM per device.

v0:
```python
import math

import jax
import jax.numpy as jnp
import numpy as np
from jax import lax
from jax.experimental import pallas as pl
from jax.experimental.pallas import tpu as pltpu
from jax.sharding import Mesh
from jax.sharding import PartitionSpec as P

LON = ("zh", "x", "c")
LAT = "lat"
LANES = 128
WIDE = 384
NB = 136
NQ = 68
NH = 72
QMAP = (0, 2, 1, 3)


def tables():
    length = 4320
    lanes = np.arange(LANES)
    group = lanes // 32
    wide_q = np.array(QMAP)[group]
    cols = np.arange(NB)
    lane_tw = np.zeros((5, 2, 8, LANES), np.float32)
    point_tw = np.zeros((5, 2, NB, LANES), np.float32)
    for p in range(5):
        a = 2 * math.pi * ((group * p) % 32) / 32
        lane_tw[p, 0] = np.cos(a)
        lane_tw[p, 1] = -np.sin(a)
        b = 2 * math.pi * ((cols[:, None] * (p + 8 * wide_q)[None]) % length) / length
        point_tw[p, 0] = np.cos(b)
        point_tw[p, 1] = -np.sin(b)
    k2 = np.zeros(2 * NH, np.int64)
    k2[:NQ] = np.arange(NQ)
    k2[NH : NH + NQ] = 134 - np.arange(NQ)
    ang = 2 * math.pi * ((k2[:, None] * np.arange(144)[None]) % 135) / 135
    mat = np.concatenate([np.cos(ang), np.sin(ang)])
    mat[:, 135:] = 0.0
    mat = mat.astype(np.float32)
    high = mat.astype(jnp.bfloat16)
    low = (mat - high.astype(np.float32)).astype(jnp.bfloat16)
    scale = np.full((1, 2176), -2.0 / length, np.float32)
    scale[0, 0] = -1.0 / length
    reverse = np.zeros((WIDE, WIDE), np.float32)
    reverse[np.arange(270), 269 - np.arange(270)] = -1.0
    return lane_tw, point_tw, high, low, scale, reverse.astype(jnp.bfloat16)


def lane_ids(rows):
    return lax.broadcasted_iota(jnp.int32, (rows, LANES), 1)


def halves(first, second):
    low = lane_ids(first.shape[0]) < 64
    a = jnp.where(low, first, pltpu.roll(second, 64, 1))
    b = jnp.where(low, pltpu.roll(first, 64, 1), second)
    return a, b


def turned(*sources):
    parts = []
    for t in range(2):
        pieces = [s[f, t, pl.ds(row, 16, stride=16), :] for s, row in sources for f in range(2)]
        parts.append(jnp.concatenate(pieces, axis=0).T)
    return parts[0], parts[1][: NB - LANES]


def mask_kernel(zh_ref, u_ref, v_ref, mu_ref, mv_ref, out_ref, first_ref, last_ref, keep_ref, send_ref, s0, s1):
    low = zh_ref[0] == 0
    zero = jnp.zeros((16, LANES), jnp.float32)
    for f, (val, msk) in enumerate(((u_ref, mu_ref), (v_ref, mv_ref))):
        for level in range(16):
            rows = slice(level * 16, level * 16 + 16)
            out_ref[f, level, :, 256:] = zero
            out_ref[f, level, :, 0:270] = val[level] * msk[level].astype(jnp.float32)
            wide = out_ref[f, level]
            later = pltpu.roll(wide, WIDE - 135, 1)
            for t in range(3):
                s0[f, t, rows, :] = wide[:, t * LANES : (t + 1) * LANES]
            for t in range(2):
                s1[f, t, rows, :] = later[:, t * LANES : (t + 1) * LANES]
        for t in range(3):
            cols = slice(t * LANES, (t + 1) * LANES)
            first_ref[f * 16 : f * 16 + 16, cols] = s0[f, t, pl.ds(0, 16, stride=16), :]
            last_ref[f * 16 : f * 16 + 16, cols] = s0[f, t, pl.ds(15, 16, stride=16), :]
    for x in range(4):
        blocks = []
        for zd in range(2):
            row = zd * 8 + x * 2
            blocks.append(turned((s0, row), (s1, row), (s0, row + 1), (s1, row + 1)))
        for part, rows in enumerate((slice(0, LANES), slice(LANES, NB))):
            keep_ref[x, rows, :] = jnp.where(low, blocks[0][part], blocks[1][part])
            send_ref[x, rows, :] = jnp.where(low, blocks[1][part], blocks[0][part])


def advect_kernel(m_ref, south_ref, north_ref, mirror_ref, t_ref, bottom_ref, dx_ref, dy_ref, reverse_ref, out_ref, tmp, s0, s1, above):
    row = lax.broadcasted_iota(jnp.int32, (16, WIDE), 0)
    lane = lax.broadcasted_iota(jnp.int32, (16, WIDE), 1)
    half_dx = 0.5 * dx_ref[...]
    half_dy = 0.5 * dy_ref[...]
    bottom = bottom_ref[...]
    rest = mirror_ref[...]
    total = north_ref[...]
    for _ in range(3):
        part = rest.astype(jnp.bfloat16)
        total = total + jnp.dot(part, reverse_ref[...], preferred_element_type=jnp.float32)
        rest = rest - part.astype(jnp.float32)
    above[...] = total
    for level in range(16):
        um = m_ref[0, level]
        vm = m_ref[1, level]
        weight = t_ref[level].astype(jnp.float32) * (level < bottom).astype(jnp.float32)
        coef_x = weight * um[:, :270] * half_dx
        coef_y = weight * vm[:, :270] * half_dy
        tmp[2, :, 0:270] = coef_x
        edge = tmp[2]
        for f, val in enumerate((um, vm)):
            at = f * 16 + level
            south = south_ref[at : at + 1, :]
            north = above[at : at + 1, :]
            up = jnp.where(row == 15, north, pltpu.roll(val, 15, 0))
            down = jnp.where(row == 0, south, pltpu.roll(val, 1, 0))
            right = pltpu.roll(val, WIDE - 1, 1)
            left = pltpu.roll(val, 1, 1)
            tmp[f, :, 0:270] = coef_x * (right - left)[:, :270] + coef_y * (up - down)[:, :270]
            adv = tmp[f]
            rows = slice(level * 16, level * 16 + 16)
            low = jnp.where(lane == 135, pltpu.roll(edge, 135, 1), adv)
            high = jnp.where(lane == 135, pltpu.roll(edge, WIDE - 134, 1), pltpu.roll(adv, WIDE - 135, 1))
            for t in range(2):
                s0[f, t, rows, :] = low[:, t * LANES : (t + 1) * LANES]
                s1[f, t, rows, :] = high[:, t * LANES : (t + 1) * LANES]
    for d in range(8):
        out_ref[d, :LANES], out_ref[d, LANES:] = turned((s0, d), (s1, d), (s0, d + 8), (s1, d + 8))


def split_kernel(zh_ref, a_ref, keep_ref, send_ref):
    low = zh_ref[0] == 0
    for x in range(4):
        a, b = halves(a_ref[2 * x], a_ref[2 * x + 1])
        keep_ref[x] = jnp.where(low, a, b)
        send_ref[x] = jnp.where(low, b, a)


def join_kernel(own_ref, other_ref, out_ref):
    for x in range(4):
        out_ref[2 * x], out_ref[2 * x + 1] = halves(own_ref[x], other_ref[x])


def transform(load, lane_tw, point_tw, high, low, work, emit):
    lane = lane_ids(8)
    sign_c = jnp.where(lane < 64, 1.0, -1.0).astype(jnp.float32)
    first_h = (lane % 64) < 32
    sign_h = jnp.where(first_h, 1.0, -1.0).astype(jnp.float32)
    turned = lane >= 96
    r = math.sqrt(0.5)

    def step(i, carry):
        rows = pl.ds(pl.multiple_of(i * 8, 8), 8)
        x = [load(j, rows, i) for j in range(8)]
        s = [x[j] + x[j + 4] for j in range(4)]
        d = [x[j] - x[j + 4] for j in range(4)]
        e0, e1 = s[0] + s[2], s[1] + s[3]
        o = r * (d[1] - d[3])
        q = r * (d[1] + d[3])
        spectrum = (
            (e0 + e1, None),
            (d[0] + o, -(d[2] + q)),
            (s[0] - s[2], s[3] - s[1]),
            (d[0] - o, d[2] - q),
            (e0 - e1, None),
        )
        for p, (re, im) in enumerate(spectrum):
            if im is None:
                if p:
                    re, im = re * lane_tw[p, 0], re * lane_tw[p, 1]
            else:
                c, t = lane_tw[p, 0], lane_tw[p, 1]
                re, im = re * c - im * t, re * t + im * c
            re = re * sign_c + pltpu.roll(re, 64, 1)
            if im is None:
                re, im = jnp.where(turned, 0.0, re), jnp.where(turned, -re, 0.0)
            else:
                im = im * sign_c + pltpu.roll(im, 64, 1)
                re, im = jnp.where(turned, im, re), jnp.where(turned, -re, im)
            re = re * sign_h + jnp.where(first_h, pltpu.roll(re, 96, 1), pltpu.roll(re, 32, 1))
            im = im * sign_h + jnp.where(first_h, pltpu.roll(im, 96, 1), pltpu.roll(im, 32, 1))
            c, t = point_tw[p, 0, rows, :], point_tw[p, 1, rows, :]
            work[p, rows, 0:LANES] = re * c - im * t
            work[p, rows, LANES : 2 * LANES] = re * t + im * c
        return carry

    lax.fori_loop(0, NB // 8, step, 0)
    for p in range(5):
        work[p, NB:144, :] = jnp.zeros((144 - NB, 2 * LANES), jnp.float32)
        full = work[p]
        full_high = full.astype(jnp.bfloat16)
        full_low = (full - full_high.astype(jnp.float32)).astype(jnp.bfloat16)
        dot = lambda a, b: jnp.dot(a, b, preferred_element_type=jnp.float32)
        g = dot(high[...], full_high) + (dot(high[...], full_low) + dot(low[...], full_high))
        cos, sin = g[: 2 * NH], g[2 * NH :]
        emit(p, cos[:, :LANES] + sin[:, LANES:], cos[:, LANES:] - sin[:, :LANES])


def velocity_kernel(a_ref, lane_tw, point_tw, high, low, re_ref, im_ref, edge_ref, blocks, work):
    for x in range(4):
        blocks[x], blocks[x + 4] = halves(a_ref[2 * x], a_ref[2 * x + 1])
    for j in range(8):
        edge_ref[j : j + 1, :] = blocks[j, 0:1, :]
        edge_ref[8 + j : 9 + j, :] = blocks[j, 134:135, :]

    def emit(p, re, im):
        re_ref[p] = re
        im_ref[p] = im

    transform(lambda j, rows, i: blocks[j, rows, :], lane_tw, point_tw, high, low, work, emit)


def flux_kernel(keep_ref, other_ref, edge_ref, fr_ref, fi_ref, lane_tw, point_tw, high, low, scale, out_ref, blocks, work, spread):
    for x in range(4):
        blocks[x] = keep_ref[x]
        blocks[x + 4] = other_ref[x]
    lane = lane_ids(1)
    first_h = (lane % 64) < 32
    for j in range(8):
        coef = blocks[j, 135:136, :]
        before = (j + 7) % 8
        after = (j + 1) % 8
        head = edge_ref[8 + j : 9 + j, :]
        head = jnp.where(lane < 32, pltpu.roll(edge_ref[8 + before : 9 + before, :], 32, 1), pltpu.roll(head, 32, 1))
        tail = edge_ref[j : j + 1, :]
        tail = jnp.where(lane >= 96, pltpu.roll(edge_ref[after : after + 1, :], 96, 1), pltpu.roll(tail, 96, 1))
        blocks[j, 0:1, :] = blocks[j, 0:1, :] - jnp.where(first_h, coef * head, 0.0)
        blocks[j, 134:135, :] = blocks[j, 134:135, :] + jnp.where(first_h, 0.0, coef * tail)

    def emit(p, re, im):
        flux = fr_ref[p] * re + fi_ref[p] * im
        flux = flux + pltpu.roll(flux, LANES - 16, 1)
        for group in range(4):
            k1 = p + 8 * QMAP[group]
            if (p == 0 and k1 == 24) or (p == 4 and k1 > 12):
                continue
            part = pltpu.roll(flux, LANES - 32 * group, 1) if group else flux
            spread[pl.ds(k1, NQ, stride=32), :] = part[:NQ]
            if k1 % 16:
                spread[pl.ds(32 - k1, NQ, stride=32), :] = part[NH : NH + NQ]

    transform(lambda j, rows, i: blocks[j, rows, :], lane_tw, point_tw, high, low, work, emit)
    for t in range(17):
        cols = slice(t * LANES, min((t + 1) * LANES, 2160))
        width = cols.stop - cols.start
        turned = spread[t * LANES : (t + 1) * LANES, :].T[:16] * scale[:, t * LANES : (t + 1) * LANES]
        out_ref[:, 0, cols] = turned[:, :width]


def result(*dims):
    return pltpu.VMEM(dims, jnp.float32)


def near(*values):
    return [pltpu.with_memory_space_constraint(v, pltpu.VMEM) for v in values]


def vmem(count):
    return [pl.BlockSpec(memory_space=pltpu.VMEM)] * count


SMEM = pl.BlockSpec(memory_space=pltpu.SMEM)


def scratch(*dims):
    return pltpu.VMEM(dims, jnp.float32)


def layer(u_vel, v_vel, u_mask, v_mask, t_mask, bottom, inv_dx, inv_dy):
    zh = lax.axis_index("zh").astype(jnp.int32).reshape(1)
    lane_tw, point_tw, high, low, scale, reverse = tables()
    masked, first, last, keep, send = pl.pallas_call(
        mask_kernel,
        out_shape=(result(2, 16, 16, WIDE), result(32, WIDE), result(32, WIDE), result(4, NB, LANES), result(4, NB, LANES)),
        in_specs=[SMEM] + vmem(4),
        out_specs=vmem(5),
        scratch_shapes=[scratch(2, 3, 256, LANES), scratch(2, 2, 256, LANES)],
    )(zh, u_vel, v_vel, u_mask, v_mask)
    other = lax.ppermute(send, "zh", [(0, 1), (1, 0)])
    count = lax.axis_size(LAT)
    ahead = [(i, i + 1) for i in range(count - 1)]
    south = lax.ppermute(last, LAT, ahead)
    north = lax.ppermute(first, LAT, [(t, s) for s, t in ahead])
    lon = lax.axis_size(LON)
    pairs = [((i + 1) * count - 1, (lon - i) * count - 1) for i in range(lon)]
    mirror = lax.ppermute(last, (*LON, LAT), pairs)
    adv = pl.pallas_call(
        advect_kernel,
        out_shape=result(8, NB, LANES),
        in_specs=vmem(9),
        out_specs=vmem(1)[0],
        scratch_shapes=[scratch(3, 16, WIDE), scratch(2, 2, 256, LANES), scratch(2, 2, 256, LANES), scratch(32, WIDE)],
    )(*near(masked, south, north, mirror), t_mask, bottom, inv_dx, inv_dy, reverse)
    adv = lax.all_to_all(adv, ("x", "c"), 0, 0, tiled=True)
    keep_adv, send_adv = pl.pallas_call(
        split_kernel,
        out_shape=(result(4, NB, LANES), result(4, NB, LANES)),
        in_specs=[SMEM] + vmem(1),
        out_specs=vmem(2),
    )(zh, *near(adv))
    other_adv = lax.ppermute(send_adv, "zh", [(0, 1), (1, 0)])
    joined = pl.pallas_call(
        join_kernel,
        out_shape=result(8, NB, LANES),
        in_specs=vmem(2),
        out_specs=vmem(1)[0],
    )(*near(keep, other))
    joined = lax.all_to_all(joined, ("x", "c"), 0, 0, tiled=True)
    re, im, edge = pl.pallas_call(
        velocity_kernel,
        out_shape=(result(5, 2 * NH, LANES), result(5, 2 * NH, LANES), result(16, LANES)),
        in_specs=vmem(5),
        out_specs=vmem(3),
        scratch_shapes=[scratch(8, NB, LANES), scratch(5, 144, 2 * LANES)],
    )(*near(joined), lane_tw, point_tw, high, low)
    return pl.pallas_call(
        flux_kernel,
        out_shape=jax.ShapeDtypeStruct((16, 1, 2160), jnp.float32),
        in_specs=vmem(10),
        out_specs=vmem(1)[0],
        scratch_shapes=[scratch(8, NB, LANES), scratch(5, 144, 2 * LANES), scratch(2176, LANES)],
    )(*near(keep_adv, other_adv, edge, re, im), lane_tw, point_tw, high, low, scale)


def solution(mesh):
    torus = Mesh(mesh.devices.reshape(2, 4, 2, mesh.shape["lat"]), ("zh", "x", "c", "lat"))
    level = P(None, "lat", LON)
    plane = P("lat", LON)
    return jax.shard_map(
        layer,
        mesh=torus,
        in_specs=(level, level, level, level, level, plane, plane, plane),
        out_specs=P(None, ("lat", *LON), None),
        check_vma=False,
    )
```

profile of v0, /device:TPU:35, one launch (start us, length us, event | category | flops | bytes accessed | tf_op | source)
XLA Modules:
  0.0 110.8 jit_solution(4483871212861878583)
XLA Ops:
  0.0 2.1 %shard_map.136 = (f32[2,16,16,384]{3,2,1,0:T(8,128)S(1)}, f32[32,384]{1,0:T(8,128)S(1)}, f32[32,384]{1,0:T(8,128)S(1)}, f32[4,136,128]{2,1,0:T(8,128)S(1)}, f32[4,136,128]{2,1,0:T(8,128)S(1)}) custom-call(s32[1]{0:T(128)} %bitcast.zh_ref, f32[16,16,270]{2,1,0:T(8,128)} %u_ref.1, f32[16,16,270]{2,1,0:T(8,128)} %v_ref.1, s32[16,16,270]{2,1,0:T(8,128)} %mu_ref.1, ...), custom_call_target="tpu_custom_call" | custom-call | tf_op jit(solution)/shard_map/pallas_call | solution.py:282
  2.1 4.2 %collective-permute-start.1 = (f32[32,384]{1,0:T(8,128)S(1)}, f32[32,384]{1,0:T(8,128)S(1)}, u32[]{:S(2)}, u32[]{:S(2)}) collective-permute-start(f32[32,384]{1,0:T(8,128)S(1)} %get-tuple-element.17), channel_id=1, source_target_pairs={{1,0},{2,1},{3,2},{4,3},{5,4},{6,5},{7,6},{8,7},{9,8},{10,9},{11,1... | collective-permute-start | bytes 147464 | tf_op jit(solution)/shard_map/ppermute | solution.py:293
  6.3 0.7 collective-permute-start.2
  6.9 1.9 %collective-permute-start = (f32[32,384]{1,0:T(8,128)S(1)}, f32[32,384]{1,0:T(8,128)S(1)}, u32[]{:S(2)}, u32[]{:S(2)}) collective-permute-start(f32[32,384]{1,0:T(8,128)S(1)} %get-tuple-element.16), channel_id=1, source_target_pairs={{0,1},{1,2},{2,3},{3,4},{4,5},{5,6},{6,7},{7,8},{8,9},{9,10},{10,1... | collective-permute-start | bytes 147464 | tf_op jit(solution)/shard_map/ppermute | solution.py:292
  8.9 0.0 collective-permute-done.1.north_ref
  8.9 0.0 collective-permute-done.2.mirror_ref
  8.9 5.0 %collective-permute-done.south_ref = f32[32,384]{1,0:T(8,128)S(1)} collective-permute-done((f32[32,384]{1,0:T(8,128)S(1)}, f32[32,384]{1,0:T(8,128)S(1)}, u32[]{:S(2)}, u32[]{:S(2)}) %collective-permute-start) | collective-permute-done | bytes 49184 | tf_op jit(solution)/shard_map/ppermute | solution.py:292
  13.9 5.1 %shard_map.137 = f32[8,136,128]{2,1,0:T(8,128)} custom-call(f32[2,16,16,384]{3,2,1,0:T(8,128)S(1)} %get-tuple-element.15.m_ref, f32[32,384]{1,0:T(8,128)S(1)} %collective-permute-done.south_ref, f32[32,384]{1,0:T(8,128)S(1)} %collective-permute-done.1.north_ref, f32[32,384]{1,0:T(8,128)S(1)} %collective-permute-done.2.mirror_ref, s32[16,16,270]{2,1,0:T(8,128)} %t_ref.1, ...), custom_call_target="tpu_custom_call" | custom-call | tf_op jit(solution)/shard_map/pallas_call | solution.py:297
  19.0 6.5 %all-to-all-start = ((f32[8,136,128]{2,1,0:T(8,128)}), f32[8,136,128]{2,1,0:T(8,128)S(1)}, u32[]{:S(2)}, u32[]{:S(2)}) async-start(f32[8,136,128]{2,1,0:T(8,128)} %shard_map.137), calls=%async_computation | async-start | bytes 1114112 | tf_op jit(solution)/shard_map/all_to_all | solution.py:304
  25.5 15.4 %collective-permute-start.4 = (f32[4,136,128]{2,1,0:T(8,128)S(1)}, f32[4,136,128]{2,1,0:T(8,128)S(1)}, u32[]{:S(2)}, u32[]{:S(2)}) collective-permute-start(f32[4,136,128]{2,1,0:T(8,128)S(1)} %get-tuple-element.21), channel_id=1, source_target_pairs={{0,256},{256,0},{1,257},{257,1},{2,258},{258,2},{3,259},{259,3},{4... | collective-permute-start | bytes 835592 | tf_op jit(solution)/shard_map/ppermute | solution.py:289
  41.0 24.6 %collective-permute-done.4.other_ref = f32[4,136,128]{2,1,0:T(8,128)S(1)} collective-permute-done((f32[4,136,128]{2,1,0:T(8,128)S(1)}, f32[4,136,128]{2,1,0:T(8,128)S(1)}, u32[]{:S(2)}, u32[]{:S(2)}) %collective-permute-start.4) | collective-permute-done | bytes 278560 | tf_op jit(solution)/shard_map/ppermute | solution.py:289
  65.5 1.0 shard_map.139
  66.5 0.0 all-to-all-done.a_ref
  66.5 5.6 %all-to-all-start.1 = ((f32[8,136,128]{2,1,0:T(8,128)}), f32[8,136,128]{2,1,0:T(8,128)S(1)}, u32[]{:S(2)}, u32[]{:S(2)}) async-start(f32[8,136,128]{2,1,0:T(8,128)} %shard_map.139), calls=%async_computation.1 | async-start | bytes 1114112 | tf_op jit(solution)/shard_map/all_to_all | solution.py:318
  72.1 0.2 shard_map.138
  72.4 11.9 %collective-permute-start.3 = (f32[4,136,128]{2,1,0:T(8,128)S(1)}, f32[4,136,128]{2,1,0:T(8,128)S(1)}, u32[]{:S(2)}, u32[]{:S(2)}) collective-permute-start(f32[4,136,128]{2,1,0:T(8,128)S(1)} %get-tuple-element.19), channel_id=1, source_target_pairs={{0,256},{256,0},{1,257},{257,1},{2,258},{258,2},{3,259},{259,3},{4... | collective-permute-start | bytes 835592 | tf_op jit(solution)/shard_map/ppermute | solution.py:311
  84.2 0.0 all-to-all-done.1.a_ref
  84.2 5.0 %shard_map.140 = (f32[5,144,128]{2,1,0:T(8,128)S(1)}, f32[5,144,128]{2,1,0:T(8,128)S(1)}, f32[16,128]{1,0:T(8,128)S(1)}) custom-call(f32[8,136,128]{2,1,0:T(8,128)S(1)} %all-to-all-done.1.a_ref, f32[5,2,8,128]{3,2,1,0:T(8,128)} %constant.19.clone.lane_tw, f32[5,2,136,128]{3,2,1,0:T(8,128)} %constant.20.clone.point_tw, bf16[288,144]{1,0:T(8,128)(2,1)} %constant.21.clone.high, ...), custom_call_target="tpu_custom_call" | custom-call | tf_op jit(solution)/shard_map/pallas_call | solution.py:319
  89.3 14.9 %collective-permute-done.3.other_ref = f32[4,136,128]{2,1,0:T(8,128)S(1)} collective-permute-done((f32[4,136,128]{2,1,0:T(8,128)S(1)}, f32[4,136,128]{2,1,0:T(8,128)S(1)}, u32[]{:S(2)}, u32[]{:S(2)}) %collective-permute-start.3) | collective-permute-done | bytes 278560 | tf_op jit(solution)/shard_map/ppermute | solution.py:311
  104.2 6.6 %shard_map.141 = f32[16,1,2160]{2,1,0:T(1,128)} custom-call(f32[4,136,128]{2,1,0:T(8,128)S(1)} %get-tuple-element.18.keep_ref, f32[4,136,128]{2,1,0:T(8,128)S(1)} %collective-permute-done.3.other_ref, f32[16,128]{1,0:T(8,128)S(1)} %get-tuple-element.22.edge_ref, f32[5,144,128]{2,1,0:T(8,128)S(1)} %get-tuple-element.23.fr_ref, ...), custom_call_target="tpu_custom_call" | custom-call | tf_op jit(solution)/shard_map/pallas_call | solution.py:326
Async XLA Ops:
  2.1 6.8 %collective-permute-start.1 = (f32[32,384]{1,0:T(8,128)S(1)}, f32[32,384]{1,0:T(8,128)S(1)}, u32[]{:S(2)}, u32[]{:S(2)}) collective-permute-start(f32[32,384]{1,0:T(8,128)S(1)} %get-tuple-element.17), channel_id=1, source_target_pairs={{1,0},{2,1},{3,2},{4,3},{5,4},{6,5},{7,6},{8,7},{9,8},{10,9},{11,1... | collective-permute-start | bytes 147464 | tf_op jit(solution)/shard_map/ppermute | solution.py:293
  6.3 2.6 %collective-permute-start.2 = (f32[32,384]{1,0:T(8,128)S(1)}, f32[32,384]{1,0:T(8,128)S(1)}, u32[]{:S(2)}, u32[]{:S(2)}) collective-permute-start(f32[32,384]{1,0:T(8,128)S(1)} %get-tuple-element.16), channel_id=1, source_target_pairs={{31,511},{63,479},{95,447},{127,415},{159,383},{191,351},{223,319}... | collective-permute-start | bytes 147464 | tf_op jit(solution)/shard_map/ppermute | solution.py:296
  6.9 6.9 %collective-permute-start = (f32[32,384]{1,0:T(8,128)S(1)}, f32[32,384]{1,0:T(8,128)S(1)}, u32[]{:S(2)}, u32[]{:S(2)}) collective-permute-start(f32[32,384]{1,0:T(8,128)S(1)} %get-tuple-element.16), channel_id=1, source_target_pairs={{0,1},{1,2},{2,3},{3,4},{4,5},{5,6},{6,7},{7,8},{8,9},{9,10},{10,1... | collective-permute-start | bytes 147464 | tf_op jit(solution)/shard_map/ppermute | solution.py:292
  19.0 47.6 %all-to-all-start = ((f32[8,136,128]{2,1,0:T(8,128)}), f32[8,136,128]{2,1,0:T(8,128)S(1)}, u32[]{:S(2)}, u32[]{:S(2)}) async-start(f32[8,136,128]{2,1,0:T(8,128)} %shard_map.137), calls=%async_computation | async-start | bytes 1114112 | tf_op jit(solution)/shard_map/all_to_all | solution.py:304
  25.5 40.0 %collective-permute-start.4 = (f32[4,136,128]{2,1,0:T(8,128)S(1)}, f32[4,136,128]{2,1,0:T(8,128)S(1)}, u32[]{:S(2)}, u32[]{:S(2)}) collective-permute-start(f32[4,136,128]{2,1,0:T(8,128)S(1)} %get-tuple-element.21), channel_id=1, source_target_pairs={{0,256},{256,0},{1,257},{257,1},{2,258},{258,2},{3,259},{259,3},{4... | collective-permute-start | bytes 835592 | tf_op jit(solution)/shard_map/ppermute | solution.py:289
  66.5 17.7 %all-to-all-start.1 = ((f32[8,136,128]{2,1,0:T(8,128)}), f32[8,136,128]{2,1,0:T(8,128)S(1)}, u32[]{:S(2)}, u32[]{:S(2)}) async-start(f32[8,136,128]{2,1,0:T(8,128)} %shard_map.139), calls=%async_computation.1 | async-start | bytes 1114112 | tf_op jit(solution)/shard_map/all_to_all | solution.py:318
  72.4 31.8 %collective-permute-start.3 = (f32[4,136,128]{2,1,0:T(8,128)S(1)}, f32[4,136,128]{2,1,0:T(8,128)S(1)}, u32[]{:S(2)}, u32[]{:S(2)}) collective-permute-start(f32[4,136,128]{2,1,0:T(8,128)S(1)} %get-tuple-element.19), channel_id=1, source_target_pairs={{0,256},{256,0},{1,257},{257,1},{2,258},{258,2},{3,259},{259,3},{4... | collective-permute-start | bytes 835592 | tf_op jit(solution)/shard_map/ppermute | solution.py:311
where the time goes:
time: 111 us
  starting transfers between devices  46.2 us (42%)
  waiting for transfers between devices  44.5 us (40%)
  Pallas kernels  20 us (18%)
    ppermute x1, waiting for transfers between devices, layer(): other = lax.ppermute(send, 'zh', [(0, 1), (1, 0)])  24.6 us
    ppermute x1, starting transfers between devices, layer(): other = lax.ppermute(send, 'zh', [(0, 1), (1, 0)])  15.4 us
    ppermute x1, waiting for transfers between devices, layer(): other_adv = lax.ppermute(send_adv, 'zh', [(0, 1), (1, 0)])  14.9 us
    ppermute x1, starting transfers between devices, layer(): other_adv = lax.ppermute(send_adv, 'zh', [(0, 1), (1, 0)])  11.9 us
    pallas_call x1, Pallas kernels, layer(): pl.pallas_call(flux_kernel, out_shape=jax.ShapeDtypeStruct((16, 1, 2160),...  6.6 us
    all_to_all x1, starting transfers between devices, layer(): adv = lax.all_to_all(adv, ('x', 'c'), 0, 0, tiled=True)  6.54 us
    all_to_all x1, starting transfers between devices, layer(): joined = lax.all_to_all(joined, ('x', 'c'), 0, 0, tiled=True)  5.59 us
    pallas_call x1, Pallas kernels, layer(): pl.pallas_call(advect_kernel, out_shape=result(8, NB, LANES), in_specs=vm...  5.11 us
  transfers between devices with their start and end apart: 7, of which 3 were waited for; matrix products, arithmetic and copies ran while one was open for 0% of the time, Pallas kernels for 6%

commit v1 on v0

--- a/solution.py
+++ b/solution.py
@@ -265,11 +265,16 @@
     return [pltpu.with_memory_space_constraint(v, pltpu.VMEM) for v in values]
 
 
+def far(*values):
+    return [pltpu.with_memory_space_constraint(v, pltpu.HBM) for v in values]
+
+
 def vmem(count):
     return [pl.BlockSpec(memory_space=pltpu.VMEM)] * count
 
 
 SMEM = pl.BlockSpec(memory_space=pltpu.SMEM)
+PARAMS = pltpu.CompilerParams(vmem_limit_bytes=16 * 2**20)
 
 
 def scratch(*dims):
@@ -278,14 +283,15 @@
 
 def layer(u_vel, v_vel, u_mask, v_mask, t_mask, bottom, inv_dx, inv_dy):
     zh = lax.axis_index("zh").astype(jnp.int32).reshape(1)
-    lane_tw, point_tw, high, low, scale, reverse = tables()
+    lane_tw, point_tw, high, low, scale, reverse = (jnp.asarray(t) for t in tables())
     masked, first, last, keep, send = pl.pallas_call(
         mask_kernel,
+        compiler_params=PARAMS,
         out_shape=(result(2, 16, 16, WIDE), result(32, WIDE), result(32, WIDE), result(4, NB, LANES), result(4, NB, LANES)),
         in_specs=[SMEM] + vmem(4),
         out_specs=vmem(5),
         scratch_shapes=[scratch(2, 3, 256, LANES), scratch(2, 2, 256, LANES)],
-    )(zh, u_vel, v_vel, u_mask, v_mask)
+    )(zh, *far(u_vel, v_vel, u_mask, v_mask))
     other = lax.ppermute(send, "zh", [(0, 1), (1, 0)])
     count = lax.axis_size(LAT)
     ahead = [(i, i + 1) for i in range(count - 1)]
@@ -296,14 +302,16 @@
     mirror = lax.ppermute(last, (*LON, LAT), pairs)
     adv = pl.pallas_call(
         advect_kernel,
+        compiler_params=PARAMS,
         out_shape=result(8, NB, LANES),
         in_specs=vmem(9),
         out_specs=vmem(1)[0],
         scratch_shapes=[scratch(3, 16, WIDE), scratch(2, 2, 256, LANES), scratch(2, 2, 256, LANES), scratch(32, WIDE)],
-    )(*near(masked, south, north, mirror), t_mask, bottom, inv_dx, inv_dy, reverse)
+    )(*near(masked, south, north, mirror, t_mask, bottom, inv_dx, inv_dy, reverse))
     adv = lax.all_to_all(adv, ("x", "c"), 0, 0, tiled=True)
     keep_adv, send_adv = pl.pallas_call(
         split_kernel,
+        compiler_params=PARAMS,
         out_shape=(result(4, NB, LANES), result(4, NB, LANES)),
         in_specs=[SMEM] + vmem(1),
         out_specs=vmem(2),
@@ -311,6 +319,7 @@
     other_adv = lax.ppermute(send_adv, "zh", [(0, 1), (1, 0)])
     joined = pl.pallas_call(
         join_kernel,
+        compiler_params=PARAMS,
         out_shape=result(8, NB, LANES),
         in_specs=vmem(2),
         out_specs=vmem(1)[0],
@@ -318,18 +327,20 @@
     joined = lax.all_to_all(joined, ("x", "c"), 0, 0, tiled=True)
     re, im, edge = pl.pallas_call(
         velocity_kernel,
+        compiler_params=PARAMS,
         out_shape=(result(5, 2 * NH, LANES), result(5, 2 * NH, LANES), result(16, LANES)),
         in_specs=vmem(5),
         out_specs=vmem(3),
         scratch_shapes=[scratch(8, NB, LANES), scratch(5, 144, 2 * LANES)],
-    )(*near(joined), lane_tw, point_tw, high, low)
+    )(*near(joined, lane_tw, point_tw, high, low))
     return pl.pallas_call(
         flux_kernel,
+        compiler_params=PARAMS,
         out_shape=jax.ShapeDtypeStruct((16, 1, 2160), jnp.float32),
         in_specs=vmem(10),
         out_specs=vmem(1)[0],
         scratch_shapes=[scratch(8, NB, LANES), scratch(5, 144, 2 * LANES), scratch(2176, LANES)],
-    )(*near(keep_adv, other_adv, edge, re, im), lane_tw, point_tw, high, low, scale)
+    )(*near(keep_adv, other_adv, edge, re, im, lane_tw, point_tw, high, low, scale))
 
 
 def solution(mesh):

time: 111 us -> 109 us (0.982)
  Pallas kernels: 20 us -> 16.6 us
    pallas_call x6, Pallas kernels: 20 us -> 16.6 us  [the longest x1 5.4 us: layer(): pl.pallas_call(flux_kernel, compiler_params=PARAMS, out_shape=jax.ShapeDt...]
    ppermute x1, waiting for transfers between devices: 14.9 us -> 16 us  [layer(): other_adv = lax.ppermute(send_adv, 'zh', [(0, 1), (1, 0)])]
  transfers between devices with their start and end apart: 7 -> 7, of which waited for: 3 -> 3; matrix products, arithmetic and copies ran while one was open for 0% -> 0% of each run, Pallas kernels for 6% -> 5%
where the time goes in v1:
time: 109 us
  starting transfers between devices  46.3 us (42%)
  waiting for transfers between devices  45.6 us (42%)
  Pallas kernels  16.6 us (15%)
    ppermute x1, waiting for transfers between devices, layer(): other = lax.ppermute(send, 'zh', [(0, 1), (1, 0)])  24.6 us
    ppermute x1, waiting for transfers between devices, layer(): other_adv = lax.ppermute(send_adv, 'zh', [(0, 1), (1, 0)])  16 us
    ppermute x1, starting transfers between devices, layer(): other = lax.ppermute(send, 'zh', [(0, 1), (1, 0)])  15.4 us
    ppermute x1, starting transfers between devices, layer(): other_adv = lax.ppermute(send_adv, 'zh', [(0, 1), (1, 0)])  11.9 us
    all_to_all x1, starting transfers between devices, layer(): adv = lax.all_to_all(adv, ('x', 'c'), 0, 0, tiled=True)  6.54 us
    all_to_all x1, starting transfers between devices, layer(): joined = lax.all_to_all(joined, ('x', 'c'), 0, 0, tiled=True)  5.73 us
    pallas_call x1, Pallas kernels, layer(): pl.pallas_call(flux_kernel, compiler_params=PARAMS, out_shape=jax.ShapeDt...  5.4 us
    ppermute x1, waiting for transfers between devices, layer(): south = lax.ppermute(last, LAT, ahead)  4.99 us
  transfers between devices with their start and end apart: 7, of which 3 were waited for; matrix products, arithmetic and copies ran while one was open for 0% of the time, Pallas kernels for 5%

profile of v1, /device:TPU:35, one launch (start us, length us, event | category | flops | bytes accessed | tf_op | source)
XLA Modules:
  0.0 108.8 jit_solution(5425506046014433745)
XLA Ops:
  0.0 0.0 copy-start.7
  0.0 0.0 copy-start.8
  0.0 2.1 %shard_map.136 = (f32[2,16,16,384]{3,2,1,0:T(8,128)S(1)}, f32[32,384]{1,0:T(8,128)S(1)}, f32[32,384]{1,0:T(8,128)S(1)}, f32[4,136,128]{2,1,0:T(8,128)S(1)}, f32[4,136,128]{2,1,0:T(8,128)S(1)}) custom-call(s32[1]{0:T(128)} %bitcast.zh_ref, f32[16,16,270]{2,1,0:T(8,128)} %u_ref.1, f32[16,16,270]{2,1,0:T(8,128)} %v_ref.1, s32[16,16,270]{2,1,0:T(8,128)} %mu_ref.1, ...), custom_call_target="tpu_custom_call" | custom-call | tf_op jit(solution)/shard_map/pallas_call | solution.py:287
  2.2 4.2 %collective-permute-start.1 = (f32[32,384]{1,0:T(8,128)S(1)}, f32[32,384]{1,0:T(8,128)S(1)}, u32[]{:S(2)}, u32[]{:S(2)}) collective-permute-start(f32[32,384]{1,0:T(8,128)S(1)} %get-tuple-element.17), channel_id=1, source_target_pairs={{1,0},{2,1},{3,2},{4,3},{5,4},{6,5},{7,6},{8,7},{9,8},{10,9},{11,1... | collective-permute-start | bytes 147464 | tf_op jit(solution)/shard_map/ppermute | solution.py:299
  6.4 0.7 collective-permute-start.2
  7.0 1.9 %collective-permute-start = (f32[32,384]{1,0:T(8,128)S(1)}, f32[32,384]{1,0:T(8,128)S(1)}, u32[]{:S(2)}, u32[]{:S(2)}) collective-permute-start(f32[32,384]{1,0:T(8,128)S(1)} %get-tuple-element.16), channel_id=1, source_target_pairs={{0,1},{1,2},{2,3},{3,4},{4,5},{5,6},{6,7},{7,8},{8,9},{9,10},{10,1... | collective-permute-start | bytes 147464 | tf_op jit(solution)/shard_map/ppermute | solution.py:298
  9.0 0.0 collective-permute-done.1.north_ref
  9.0 0.0 collective-permute-done.2.mirror_ref
  9.0 5.0 %collective-permute-done.south_ref = f32[32,384]{1,0:T(8,128)S(1)} collective-permute-done((f32[32,384]{1,0:T(8,128)S(1)}, f32[32,384]{1,0:T(8,128)S(1)}, u32[]{:S(2)}, u32[]{:S(2)}) %collective-permute-start) | collective-permute-done | bytes 49184 | tf_op jit(solution)/shard_map/ppermute | solution.py:298
  14.0 0.0 copy-done.3
  14.0 0.0 copy-done.4
  14.0 0.0 copy-done.6
  14.0 0.0 copy-done.7
  14.0 0.0 copy-done.8
  14.0 4.0 %shard_map.137 = f32[8,136,128]{2,1,0:T(8,128)} custom-call(f32[2,16,16,384]{3,2,1,0:T(8,128)S(1)} %get-tuple-element.15.m_ref, f32[32,384]{1,0:T(8,128)S(1)} %collective-permute-done.south_ref, f32[32,384]{1,0:T(8,128)S(1)} %collective-permute-done.1.north_ref, f32[32,384]{1,0:T(8,128)S(1)} %collective-permute-done.2.mirror_ref, ...), custom_call_target="tpu_custom_call" | custom-call | tf_op jit(solution)/shard_map/pallas_call | solution.py:303
  18.0 6.5 %all-to-all-start = ((f32[8,136,128]{2,1,0:T(8,128)}), f32[8,136,128]{2,1,0:T(8,128)S(1)}, u32[]{:S(2)}, u32[]{:S(2)}) async-start(f32[8,136,128]{2,1,0:T(8,128)} %shard_map.137), calls=%async_computation | async-start | bytes 1114112 | tf_op jit(solution)/shard_map/all_to_all | solution.py:311
  24.6 15.4 %collective-permute-start.4 = (f32[4,136,128]{2,1,0:T(8,128)S(1)}, f32[4,136,128]{2,1,0:T(8,128)S(1)}, u32[]{:S(2)}, u32[]{:S(2)}) collective-permute-start(f32[4,136,128]{2,1,0:T(8,128)S(1)} %get-tuple-element.21), channel_id=1, source_target_pairs={{0,256},{256,0},{1,257},{257,1},{2,258},{258,2},{3,259},{259,3},{4... | collective-permute-start | bytes 835592 | tf_op jit(solution)/shard_map/ppermute | solution.py:295
  40.0 24.6 %collective-permute-done.4.other_ref = f32[4,136,128]{2,1,0:T(8,128)S(1)} collective-permute-done((f32[4,136,128]{2,1,0:T(8,128)S(1)}, f32[4,136,128]{2,1,0:T(8,128)S(1)}, u32[]{:S(2)}, u32[]{:S(2)}) %collective-permute-start.4) | collective-permute-done | bytes 278560 | tf_op jit(solution)/shard_map/ppermute | solution.py:295
  64.6 1.0 shard_map.139
  65.6 0.0 all-to-all-done.a_ref
  65.6 5.7 %all-to-all-start.1 = ((f32[8,136,128]{2,1,0:T(8,128)}), f32[8,136,128]{2,1,0:T(8,128)S(1)}, u32[]{:S(2)}, u32[]{:S(2)}) async-start(f32[8,136,128]{2,1,0:T(8,128)} %shard_map.139), calls=%async_computation.1 | async-start | bytes 1114112 | tf_op jit(solution)/shard_map/all_to_all | solution.py:327
  71.3 0.2 shard_map.138
  71.6 11.9 %collective-permute-start.3 = (f32[4,136,128]{2,1,0:T(8,128)S(1)}, f32[4,136,128]{2,1,0:T(8,128)S(1)}, u32[]{:S(2)}, u32[]{:S(2)}) collective-permute-start(f32[4,136,128]{2,1,0:T(8,128)S(1)} %get-tuple-element.19), channel_id=1, source_target_pairs={{0,256},{256,0},{1,257},{257,1},{2,258},{258,2},{3,259},{259,3},{4... | collective-permute-start | bytes 835592 | tf_op jit(solution)/shard_map/ppermute | solution.py:319
  83.4 0.0 all-to-all-done.1.a_ref
  83.5 0.0 copy-done
  83.5 0.0 copy-done.1
  83.5 0.0 copy-done.2
  83.5 0.0 copy-done.5
  83.5 0.0 copy-start.9
  83.5 3.8 %shard_map.140 = (f32[5,144,128]{2,1,0:T(8,128)S(1)}, f32[5,144,128]{2,1,0:T(8,128)S(1)}, f32[16,128]{1,0:T(8,128)S(1)}) custom-call(f32[8,136,128]{2,1,0:T(8,128)S(1)} %all-to-all-done.1.a_ref, f32[5,2,8,128]{3,2,1,0:T(8,128)S(1)} %copy-done.5, f32[5,2,136,128]{3,2,1,0:T(8,128)S(1)} %copy-done, bf16[288,144]{1,0:T(8,128)(2,1)S(1)} %copy-done.2, ...), custom_call_target="tpu_custom_call" | custom-call | tf_op jit(solution)/shard_map/pallas_call | solution.py:328
  87.3 16.0 %collective-permute-done.3.other_ref = f32[4,136,128]{2,1,0:T(8,128)S(1)} collective-permute-done((f32[4,136,128]{2,1,0:T(8,128)S(1)}, f32[4,136,128]{2,1,0:T(8,128)S(1)}, u32[]{:S(2)}, u32[]{:S(2)}) %collective-permute-start.3) | collective-permute-done | bytes 278560 | tf_op jit(solution)/shard_map/ppermute | solution.py:319
  103.4 5.4 %shard_map.141 = f32[16,1,2160]{2,1,0:T(1,128)} custom-call(f32[4,136,128]{2,1,0:T(8,128)S(1)} %get-tuple-element.18.keep_ref, f32[4,136,128]{2,1,0:T(8,128)S(1)} %collective-permute-done.3.other_ref, f32[16,128]{1,0:T(8,128)S(1)} %get-tuple-element.22.edge_ref, f32[5,144,128]{2,1,0:T(8,128)S(1)} %get-tuple-element.23.fr_ref, ...), custom_call_target="tpu_custom_call" | custom-call | tf_op jit(solution)/shard_map/pallas_call | solution.py:336
  (8 shorter events, 0.0 us)
Async XLA Ops:
  0.0 14.0 %copy-start.3 = (s32[16,16,270]{2,1,0:T(8,128)S(1)}, s32[16,16,270]{2,1,0:T(8,128)}, u32[]{:S(2)}) copy-start(s32[16,16,270]{2,1,0:T(8,128)} %t_ref.1) | copy-start | bytes 829444
  0.0 14.0 %copy-start.4 = (bf16[384,384]{1,0:T(8,128)(2,1)S(1)}, bf16[384,384]{1,0:T(8,128)(2,1)}, u32[]{:S(2)}) copy-start(bf16[384,384]{1,0:T(8,128)(2,1)} %constant.23.clone.reverse_ref) | copy-start | bytes 884740
  0.0 14.0 %copy-start.6 = (s32[16,270]{1,0:T(8,128)S(1)}, s32[16,270]{1,0:T(8,128)}, u32[]{:S(2)}) copy-start(s32[16,270]{1,0:T(8,128)} %bottom_ref.1) | copy-start | bytes 51844
  0.0 14.0 %copy-start.7 = (f32[16,270]{1,0:T(8,128)S(1)}, f32[16,270]{1,0:T(8,128)}, u32[]{:S(2)}) copy-start(f32[16,270]{1,0:T(8,128)} %dx_ref.1) | copy-start | bytes 51844
  0.0 14.0 %copy-start.8 = (f32[16,270]{1,0:T(8,128)S(1)}, f32[16,270]{1,0:T(8,128)}, u32[]{:S(2)}) copy-start(f32[16,270]{1,0:T(8,128)} %dy_ref.1) | copy-start | bytes 51844
  2.2 6.8 %collective-permute-start.1 = (f32[32,384]{1,0:T(8,128)S(1)}, f32[32,384]{1,0:T(8,128)S(1)}, u32[]{:S(2)}, u32[]{:S(2)}) collective-permute-start(f32[32,384]{1,0:T(8,128)S(1)} %get-tuple-element.17), channel_id=1, source_target_pairs={{1,0},{2,1},{3,2},{4,3},{5,4},{6,5},{7,6},{8,7},{9,8},{10,9},{11,1... | collective-permute-start | bytes 147464 | tf_op jit(solution)/shard_map/ppermute | solution.py:299
  6.4 2.6 %collective-permute-start.2 = (f32[32,384]{1,0:T(8,128)S(1)}, f32[32,384]{1,0:T(8,128)S(1)}, u32[]{:S(2)}, u32[]{:S(2)}) collective-permute-start(f32[32,384]{1,0:T(8,128)S(1)} %get-tuple-element.16), channel_id=1, source_target_pairs={{31,511},{63,479},{95,447},{127,415},{159,383},{191,351},{223,319}... | collective-permute-start | bytes 147464 | tf_op jit(solution)/shard_map/ppermute | solution.py:302
  7.0 6.9 %collective-permute-start = (f32[32,384]{1,0:T(8,128)S(1)}, f32[32,384]{1,0:T(8,128)S(1)}, u32[]{:S(2)}, u32[]{:S(2)}) collective-permute-start(f32[32,384]{1,0:T(8,128)S(1)} %get-tuple-element.16), channel_id=1, source_target_pairs={{0,1},{1,2},{2,3},{3,4},{4,5},{5,6},{6,7},{7,8},{8,9},{9,10},{10,1... | collective-permute-start | bytes 147464 | tf_op jit(solution)/shard_map/ppermute | solution.py:298
  18.0 47.6 %all-to-all-start = ((f32[8,136,128]{2,1,0:T(8,128)}), f32[8,136,128]{2,1,0:T(8,128)S(1)}, u32[]{:S(2)}, u32[]{:S(2)}) async-start(f32[8,136,128]{2,1,0:T(8,128)} %shard_map.137), calls=%async_computation | async-start | bytes 1114112 | tf_op jit(solution)/shard_map/all_to_all | solution.py:311
  24.6 40.0 %collective-permute-start.4 = (f32[4,136,128]{2,1,0:T(8,128)S(1)}, f32[4,136,128]{2,1,0:T(8,128)S(1)}, u32[]{:S(2)}, u32[]{:S(2)}) collective-permute-start(f32[4,136,128]{2,1,0:T(8,128)S(1)} %get-tuple-element.21), channel_id=1, source_target_pairs={{0,256},{256,0},{1,257},{257,1},{2,258},{258,2},{3,259},{259,3},{4... | collective-permute-start | bytes 835592 | tf_op jit(solution)/shard_map/ppermute | solution.py:295
  65.6 17.9 %copy-start = (f32[5,2,136,128]{3,2,1,0:T(8,128)S(1)}, f32[5,2,136,128]{3,2,1,0:T(8,128)}, u32[]{:S(2)}) copy-start(f32[5,2,136,128]{3,2,1,0:T(8,128)} %constant.19.clone.point_tw) | copy-start | bytes 2088964
  65.6 17.8 %all-to-all-start.1 = ((f32[8,136,128]{2,1,0:T(8,128)}), f32[8,136,128]{2,1,0:T(8,128)S(1)}, u32[]{:S(2)}, u32[]{:S(2)}) async-start(f32[8,136,128]{2,1,0:T(8,128)} %shard_map.139), calls=%async_computation.1 | async-start | bytes 1114112 | tf_op jit(solution)/shard_map/all_to_all | solution.py:327
  71.3 12.1 %copy-start.1 = (bf16[288,144]{1,0:T(8,128)(2,1)S(1)}, bf16[288,144]{1,0:T(8,128)(2,1)}, u32[]{:S(2)}) copy-start(bf16[288,144]{1,0:T(8,128)(2,1)} %constant.21.clone.low) | copy-start | bytes 248836
  71.3 12.1 %copy-start.2 = (bf16[288,144]{1,0:T(8,128)(2,1)S(1)}, bf16[288,144]{1,0:T(8,128)(2,1)}, u32[]{:S(2)}) copy-start(bf16[288,144]{1,0:T(8,128)(2,1)} %constant.20.clone.high) | copy-start | bytes 248836
  71.3 12.2 %copy-start.5 = (f32[5,2,8,128]{3,2,1,0:T(8,128)S(1)}, f32[5,2,8,128]{3,2,1,0:T(8,128)}, u32[]{:S(2)}) copy-start(f32[5,2,8,128]{3,2,1,0:T(8,128)} %constant.18.clone.lane_tw) | copy-start | bytes 122884
  71.6 31.8 %collective-permute-start.3 = (f32[4,136,128]{2,1,0:T(8,128)S(1)}, f32[4,136,128]{2,1,0:T(8,128)S(1)}, u32[]{:S(2)}, u32[]{:S(2)}) collective-permute-start(f32[4,136,128]{2,1,0:T(8,128)S(1)} %get-tuple-element.19), channel_id=1, source_target_pairs={{0,256},{256,0},{1,257},{257,1},{2,258},{258,2},{3,259},{259,3},{4... | collective-permute-start | bytes 835592 | tf_op jit(solution)/shard_map/ppermute | solution.py:319
  83.5 19.9 %copy-start.9 = (f32[1,2176]{1,0:T(1,128)S(1)}, f32[1,2176]{1,0:T(1,128)}, u32[]{:S(2)}) copy-start(f32[1,2176]{1,0:T(1,128)} %constant.22.clone.scale) | copy-start | bytes 26116

commit v2 on v1

--- a/solution.py
+++ b/solution.py
@@ -17,6 +17,8 @@
 NQ = 68
 NH = 72
 QMAP = (0, 2, 1, 3)
+PITCH = 40
+UNROLL = 4
 
 
 def tables():
@@ -194,7 +196,7 @@
             work[p, rows, LANES : 2 * LANES] = re * t + im * c
         return carry
 
-    lax.fori_loop(0, NB // 8, step, 0)
+    lax.fori_loop(0, NB // 8, step, 0, unroll=UNROLL)
     for p in range(5):
         work[p, NB:144, :] = jnp.zeros((144 - NB, 2 * LANES), jnp.float32)
         full = work[p]
@@ -245,16 +247,16 @@
             if (p == 0 and k1 == 24) or (p == 4 and k1 > 12):
                 continue
             part = pltpu.roll(flux, LANES - 32 * group, 1) if group else flux
-            spread[pl.ds(k1, NQ, stride=32), :] = part[:NQ]
+            spread[pl.ds(k1, NQ, stride=PITCH), :] = part[:NQ]
             if k1 % 16:
-                spread[pl.ds(32 - k1, NQ, stride=32), :] = part[NH : NH + NQ]
+                spread[pl.ds(32 - k1, NQ, stride=PITCH), :] = part[NH : NH + NQ]
 
     transform(lambda j, rows, i: blocks[j, rows, :], lane_tw, point_tw, high, low, work, emit)
     for t in range(17):
         cols = slice(t * LANES, min((t + 1) * LANES, 2160))
-        width = cols.stop - cols.start
-        turned = spread[t * LANES : (t + 1) * LANES, :].T[:16] * scale[:, t * LANES : (t + 1) * LANES]
-        out_ref[:, 0, cols] = turned[:, :width]
+        pieces = [spread[k2 * PITCH : k2 * PITCH + 32, :] for k2 in range(4 * t, 4 * t + 4)]
+        piece = jnp.concatenate(pieces, axis=0).T[:16] * scale[:, t * LANES : (t + 1) * LANES]
+        out_ref[:, 0, cols] = piece[:, : cols.stop - cols.start]
 
 
 def result(*dims):
@@ -339,7 +341,7 @@
         out_shape=jax.ShapeDtypeStruct((16, 1, 2160), jnp.float32),
         in_specs=vmem(10),
         out_specs=vmem(1)[0],
-        scratch_shapes=[scratch(8, NB, LANES), scratch(5, 144, 2 * LANES), scratch(2176, LANES)],
+        scratch_shapes=[scratch(8, NB, LANES), scratch(5, 144, 2 * LANES), scratch(NQ * PITCH, LANES)],
     )(*near(keep_adv, other_adv, edge, re, im, lane_tw, point_tw, high, low, scale))
 
 

time: 109 us -> 107 us (0.982)
  Pallas kernels: 16.6 us -> 12.6 us
  waiting for transfers between devices: 45.6 us -> 47.4 us
    pallas_call x1, Pallas kernels: 5.4 us -> 3.11 us  [layer(): pl.pallas_call(flux_kernel, compiler_params=PARAMS, out_shape=jax.ShapeDt...]
    ppermute x1, waiting for transfers between devices: 16 us -> 17.8 us  [layer(): other_adv = lax.ppermute(send_adv, 'zh', [(0, 1), (1, 0)])]
    pallas_call x1, Pallas kernels: 3.83 us -> 2.05 us  [layer(): pl.pallas_call(velocity_kernel, compiler_params=PARAMS, out_shape=(result...]
  transfers between devices with their start and end apart: 7 -> 7, of which waited for: 3 -> 3; matrix products, arithmetic and copies ran while one was open for 0% -> 0% of each run, Pallas kernels for 5% -> 3%
where the time goes in v2:
time: 107 us; the launch traced here: 106 us
  waiting for transfers between devices  47.4 us (44%)
  starting transfers between devices  46.3 us (43%)
  Pallas kernels  12.6 us (12%)
    ppermute x1, waiting for transfers between devices, layer(): other = lax.ppermute(send, 'zh', [(0, 1), (1, 0)])  24.6 us
    ppermute x1, waiting for transfers between devices, layer(): other_adv = lax.ppermute(send_adv, 'zh', [(0, 1), (1, 0)])  17.8 us
    ppermute x1, starting transfers between devices, layer(): other = lax.ppermute(send, 'zh', [(0, 1), (1, 0)])  15.4 us
    ppermute x1, starting transfers between devices, layer(): other_adv = lax.ppermute(send_adv, 'zh', [(0, 1), (1, 0)])  11.9 us
    all_to_all x1, starting transfers between devices, layer(): adv = lax.all_to_all(adv, ('x', 'c'), 0, 0, tiled=True)  6.54 us
    all_to_all x1, starting transfers between devices, layer(): joined = lax.all_to_all(joined, ('x', 'c'), 0, 0, tiled=True)  5.73 us
    ppermute x1, waiting for transfers between devices, layer(): south = lax.ppermute(last, LAT, ahead)  4.99 us
    ppermute x1, starting transfers between devices, layer(): north = lax.ppermute(first, LAT, [(t, s) for s, t in ahead])  4.19 us
  transfers between devices with their start and end apart: 7, of which 3 were waited for; matrix products, arithmetic and copies ran while one was open for 0% of the time, Pallas kernels for 3%

profile of v2, /device:TPU:35, one launch (start us, length us, event | category | flops | bytes accessed | tf_op | source)
XLA Modules:
  0.0 106.5 jit_solution(17721437323782529720)
XLA Ops:
  0.0 0.0 copy-start.7
  0.0 0.0 copy-start.8
  0.0 2.1 %shard_map.136 = (f32[2,16,16,384]{3,2,1,0:T(8,128)S(1)}, f32[32,384]{1,0:T(8,128)S(1)}, f32[32,384]{1,0:T(8,128)S(1)}, f32[4,136,128]{2,1,0:T(8,128)S(1)}, f32[4,136,128]{2,1,0:T(8,128)S(1)}) custom-call(s32[1]{0:T(128)} %bitcast.zh_ref, f32[16,16,270]{2,1,0:T(8,128)} %u_ref.1, f32[16,16,270]{2,1,0:T(8,128)} %v_ref.1, s32[16,16,270]{2,1,0:T(8,128)} %mu_ref.1, ...), custom_call_target="tpu_custom_call" | custom-call | tf_op jit(solution)/shard_map/pallas_call | solution.py:289
  2.2 4.2 %collective-permute-start.1 = (f32[32,384]{1,0:T(8,128)S(1)}, f32[32,384]{1,0:T(8,128)S(1)}, u32[]{:S(2)}, u32[]{:S(2)}) collective-permute-start(f32[32,384]{1,0:T(8,128)S(1)} %get-tuple-element.17), channel_id=1, source_target_pairs={{1,0},{2,1},{3,2},{4,3},{5,4},{6,5},{7,6},{8,7},{9,8},{10,9},{11,1... | collective-permute-start | bytes 147464 | tf_op jit(solution)/shard_map/ppermute | solution.py:301
  6.4 0.7 collective-permute-start.2
  7.0 1.9 %collective-permute-start = (f32[32,384]{1,0:T(8,128)S(1)}, f32[32,384]{1,0:T(8,128)S(1)}, u32[]{:S(2)}, u32[]{:S(2)}) collective-permute-start(f32[32,384]{1,0:T(8,128)S(1)} %get-tuple-element.16), channel_id=1, source_target_pairs={{0,1},{1,2},{2,3},{3,4},{4,5},{5,6},{6,7},{7,8},{8,9},{9,10},{10,1... | collective-permute-start | bytes 147464 | tf_op jit(solution)/shard_map/ppermute | solution.py:300
  9.0 0.0 collective-permute-done.1.north_ref
  9.0 0.0 collective-permute-done.2.mirror_ref
  9.0 5.0 %collective-permute-done.south_ref = f32[32,384]{1,0:T(8,128)S(1)} collective-permute-done((f32[32,384]{1,0:T(8,128)S(1)}, f32[32,384]{1,0:T(8,128)S(1)}, u32[]{:S(2)}, u32[]{:S(2)}) %collective-permute-start) | collective-permute-done | bytes 49184 | tf_op jit(solution)/shard_map/ppermute | solution.py:300
  14.0 0.0 copy-done.3
  14.0 0.0 copy-done.4
  14.0 0.0 copy-done.6
  14.0 0.0 copy-done.7
  14.0 0.0 copy-done.8
  14.0 4.0 %shard_map.137 = f32[8,136,128]{2,1,0:T(8,128)} custom-call(f32[2,16,16,384]{3,2,1,0:T(8,128)S(1)} %get-tuple-element.15.m_ref, f32[32,384]{1,0:T(8,128)S(1)} %collective-permute-done.south_ref, f32[32,384]{1,0:T(8,128)S(1)} %collective-permute-done.1.north_ref, f32[32,384]{1,0:T(8,128)S(1)} %collective-permute-done.2.mirror_ref, ...), custom_call_target="tpu_custom_call" | custom-call | tf_op jit(solution)/shard_map/pallas_call | solution.py:305
  18.0 6.5 %all-to-all-start = ((f32[8,136,128]{2,1,0:T(8,128)}), f32[8,136,128]{2,1,0:T(8,128)S(1)}, u32[]{:S(2)}, u32[]{:S(2)}) async-start(f32[8,136,128]{2,1,0:T(8,128)} %shard_map.137), calls=%async_computation | async-start | bytes 1114112 | tf_op jit(solution)/shard_map/all_to_all | solution.py:313
  24.6 15.4 %collective-permute-start.4 = (f32[4,136,128]{2,1,0:T(8,128)S(1)}, f32[4,136,128]{2,1,0:T(8,128)S(1)}, u32[]{:S(2)}, u32[]{:S(2)}) collective-permute-start(f32[4,136,128]{2,1,0:T(8,128)S(1)} %get-tuple-element.21), channel_id=1, source_target_pairs={{0,256},{256,0},{1,257},{257,1},{2,258},{258,2},{3,259},{259,3},{4... | collective-permute-start | bytes 835592 | tf_op jit(solution)/shard_map/ppermute | solution.py:297
  40.0 24.6 %collective-permute-done.4.other_ref = f32[4,136,128]{2,1,0:T(8,128)S(1)} collective-permute-done((f32[4,136,128]{2,1,0:T(8,128)S(1)}, f32[4,136,128]{2,1,0:T(8,128)S(1)}, u32[]{:S(2)}, u32[]{:S(2)}) %collective-permute-start.4) | collective-permute-done | bytes 278560 | tf_op jit(solution)/shard_map/ppermute | solution.py:297
  64.6 1.0 shard_map.139
  65.6 0.0 all-to-all-done.a_ref
  65.6 5.7 %all-to-all-start.1 = ((f32[8,136,128]{2,1,0:T(8,128)}), f32[8,136,128]{2,1,0:T(8,128)S(1)}, u32[]{:S(2)}, u32[]{:S(2)}) async-start(f32[8,136,128]{2,1,0:T(8,128)} %shard_map.139), calls=%async_computation.1 | async-start | bytes 1114112 | tf_op jit(solution)/shard_map/all_to_all | solution.py:329
  71.3 0.2 shard_map.138
  71.6 11.9 %collective-permute-start.3 = (f32[4,136,128]{2,1,0:T(8,128)S(1)}, f32[4,136,128]{2,1,0:T(8,128)S(1)}, u32[]{:S(2)}, u32[]{:S(2)}) collective-permute-start(f32[4,136,128]{2,1,0:T(8,128)S(1)} %get-tuple-element.19), channel_id=1, source_target_pairs={{0,256},{256,0},{1,257},{257,1},{2,258},{258,2},{3,259},{259,3},{4... | collective-permute-start | bytes 835592 | tf_op jit(solution)/shard_map/ppermute | solution.py:321
  83.4 0.0 all-to-all-done.1.a_ref
  83.5 0.0 copy-done
  83.5 0.0 copy-done.1
  83.5 0.0 copy-done.2
  83.5 0.0 copy-done.5
  83.5 0.0 copy-start.9
  83.5 2.1 %shard_map.140 = (f32[5,144,128]{2,1,0:T(8,128)S(1)}, f32[5,144,128]{2,1,0:T(8,128)S(1)}, f32[16,128]{1,0:T(8,128)S(1)}) custom-call(f32[8,136,128]{2,1,0:T(8,128)S(1)} %all-to-all-done.1.a_ref, f32[5,2,8,128]{3,2,1,0:T(8,128)S(1)} %copy-done.5, f32[5,2,136,128]{3,2,1,0:T(8,128)S(1)} %copy-done, bf16[288,144]{1,0:T(8,128)(2,1)S(1)} %copy-done.2, ...), custom_call_target="tpu_custom_call" | custom-call | tf_op jit(solution)/shard_map/pallas_call | solution.py:330
  85.6 17.8 %collective-permute-done.3.other_ref = f32[4,136,128]{2,1,0:T(8,128)S(1)} collective-permute-done((f32[4,136,128]{2,1,0:T(8,128)S(1)}, f32[4,136,128]{2,1,0:T(8,128)S(1)}, u32[]{:S(2)}, u32[]{:S(2)}) %collective-permute-start.3) | collective-permute-done | bytes 278560 | tf_op jit(solution)/shard_map/ppermute | solution.py:321
  103.4 3.1 %shard_map.141 = f32[16,1,2160]{2,1,0:T(1,128)} custom-call(f32[4,136,128]{2,1,0:T(8,128)S(1)} %get-tuple-element.18.keep_ref, f32[4,136,128]{2,1,0:T(8,128)S(1)} %collective-permute-done.3.other_ref, f32[16,128]{1,0:T(8,128)S(1)} %get-tuple-element.22.edge_ref, f32[5,144,128]{2,1,0:T(8,128)S(1)} %get-tuple-element.23.fr_ref, ...), custom_call_target="tpu_custom_call" | custom-call | tf_op jit(solution)/shard_map/pallas_call | solution.py:338
  (8 shorter events, 0.0 us)
Async XLA Ops:
  0.0 14.0 %copy-start.3 = (s32[16,16,270]{2,1,0:T(8,128)S(1)}, s32[16,16,270]{2,1,0:T(8,128)}, u32[]{:S(2)}) copy-start(s32[16,16,270]{2,1,0:T(8,128)} %t_ref.1) | copy-start | bytes 829444
  0.0 14.0 %copy-start.4 = (bf16[384,384]{1,0:T(8,128)(2,1)S(1)}, bf16[384,384]{1,0:T(8,128)(2,1)}, u32[]{:S(2)}) copy-start(bf16[384,384]{1,0:T(8,128)(2,1)} %constant.23.clone.reverse_ref) | copy-start | bytes 884740
  0.0 14.0 %copy-start.6 = (s32[16,270]{1,0:T(8,128)S(1)}, s32[16,270]{1,0:T(8,128)}, u32[]{:S(2)}) copy-start(s32[16,270]{1,0:T(8,128)} %bottom_ref.1) | copy-start | bytes 51844
  0.0 14.0 %copy-start.7 = (f32[16,270]{1,0:T(8,128)S(1)}, f32[16,270]{1,0:T(8,128)}, u32[]{:S(2)}) copy-start(f32[16,270]{1,0:T(8,128)} %dx_ref.1) | copy-start | bytes 51844
  0.0 14.0 %copy-start.8 = (f32[16,270]{1,0:T(8,128)S(1)}, f32[16,270]{1,0:T(8,128)}, u32[]{:S(2)}) copy-start(f32[16,270]{1,0:T(8,128)} %dy_ref.1) | copy-start | bytes 51844
  2.2 6.8 %collective-permute-start.1 = (f32[32,384]{1,0:T(8,128)S(1)}, f32[32,384]{1,0:T(8,128)S(1)}, u32[]{:S(2)}, u32[]{:S(2)}) collective-permute-start(f32[32,384]{1,0:T(8,128)S(1)} %get-tuple-element.17), channel_id=1, source_target_pairs={{1,0},{2,1},{3,2},{4,3},{5,4},{6,5},{7,6},{8,7},{9,8},{10,9},{11,1... | collective-permute-start | bytes 147464 | tf_op jit(solution)/shard_map/ppermute | solution.py:301
  6.4 2.6 %collective-permute-start.2 = (f32[32,384]{1,0:T(8,128)S(1)}, f32[32,384]{1,0:T(8,128)S(1)}, u32[]{:S(2)}, u32[]{:S(2)}) collective-permute-start(f32[32,384]{1,0:T(8,128)S(1)} %get-tuple-element.16), channel_id=1, source_target_pairs={{31,511},{63,479},{95,447},{127,415},{159,383},{191,351},{223,319}... | collective-permute-start | bytes 147464 | tf_op jit(solution)/shard_map/ppermute | solution.py:304
  7.0 6.9 %collective-permute-start = (f32[32,384]{1,0:T(8,128)S(1)}, f32[32,384]{1,0:T(8,128)S(1)}, u32[]{:S(2)}, u32[]{:S(2)}) collective-permute-start(f32[32,384]{1,0:T(8,128)S(1)} %get-tuple-element.16), channel_id=1, source_target_pairs={{0,1},{1,2},{2,3},{3,4},{4,5},{5,6},{6,7},{7,8},{8,9},{9,10},{10,1... | collective-permute-start | bytes 147464 | tf_op jit(solution)/shard_map/ppermute | solution.py:300
  18.0 47.6 %all-to-all-start = ((f32[8,136,128]{2,1,0:T(8,128)}), f32[8,136,128]{2,1,0:T(8,128)S(1)}, u32[]{:S(2)}, u32[]{:S(2)}) async-start(f32[8,136,128]{2,1,0:T(8,128)} %shard_map.137), calls=%async_computation | async-start | bytes 1114112 | tf_op jit(solution)/shard_map/all_to_all | solution.py:313
  24.6 40.0 %collective-permute-start.4 = (f32[4,136,128]{2,1,0:T(8,128)S(1)}, f32[4,136,128]{2,1,0:T(8,128)S(1)}, u32[]{:S(2)}, u32[]{:S(2)}) collective-permute-start(f32[4,136,128]{2,1,0:T(8,128)S(1)} %get-tuple-element.21), channel_id=1, source_target_pairs={{0,256},{256,0},{1,257},{257,1},{2,258},{258,2},{3,259},{259,3},{4... | collective-permute-start | bytes 835592 | tf_op jit(solution)/shard_map/ppermute | solution.py:297
  65.6 17.9 %copy-start = (f32[5,2,136,128]{3,2,1,0:T(8,128)S(1)}, f32[5,2,136,128]{3,2,1,0:T(8,128)}, u32[]{:S(2)}) copy-start(f32[5,2,136,128]{3,2,1,0:T(8,128)} %constant.19.clone.point_tw) | copy-start | bytes 2088964
  65.6 17.8 %all-to-all-start.1 = ((f32[8,136,128]{2,1,0:T(8,128)}), f32[8,136,128]{2,1,0:T(8,128)S(1)}, u32[]{:S(2)}, u32[]{:S(2)}) async-start(f32[8,136,128]{2,1,0:T(8,128)} %shard_map.139), calls=%async_computation.1 | async-start | bytes 1114112 | tf_op jit(solution)/shard_map/all_to_all | solution.py:329
  71.3 12.1 %copy-start.1 = (bf16[288,144]{1,0:T(8,128)(2,1)S(1)}, bf16[288,144]{1,0:T(8,128)(2,1)}, u32[]{:S(2)}) copy-start(bf16[288,144]{1,0:T(8,128)(2,1)} %constant.21.clone.low) | copy-start | bytes 248836
  71.3 12.1 %copy-start.2 = (bf16[288,144]{1,0:T(8,128)(2,1)S(1)}, bf16[288,144]{1,0:T(8,128)(2,1)}, u32[]{:S(2)}) copy-start(bf16[288,144]{1,0:T(8,128)(2,1)} %constant.20.clone.high) | copy-start | bytes 248836
  71.3 12.2 %copy-start.5 = (f32[5,2,8,128]{3,2,1,0:T(8,128)S(1)}, f32[5,2,8,128]{3,2,1,0:T(8,128)}, u32[]{:S(2)}) copy-start(f32[5,2,8,128]{3,2,1,0:T(8,128)} %constant.18.clone.lane_tw) | copy-start | bytes 122884
  71.6 31.8 %collective-permute-start.3 = (f32[4,136,128]{2,1,0:T(8,128)S(1)}, f32[4,136,128]{2,1,0:T(8,128)S(1)}, u32[]{:S(2)}, u32[]{:S(2)}) collective-permute-start(f32[4,136,128]{2,1,0:T(8,128)S(1)} %get-tuple-element.19), channel_id=1, source_target_pairs={{0,256},{256,0},{1,257},{257,1},{2,258},{258,2},{3,259},{259,3},{4... | collective-permute-start | bytes 835592 | tf_op jit(solution)/shard_map/ppermute | solution.py:321
  83.5 19.9 %copy-start.9 = (f32[1,2176]{1,0:T(1,128)S(1)}, f32[1,2176]{1,0:T(1,128)}, u32[]{:S(2)}) copy-start(f32[1,2176]{1,0:T(1,128)} %constant.22.clone.scale) | copy-start | bytes 26116
